TPU v7x, 512 devices: a whole 4x8x8 slice. The times are simulated.
512 devices in a mesh: row: 32 (over z, x), col: 16 (over y, core).
Axes of the slice: x: 4, y: 8, z: 8, core: 2. Of those that a mesh axis runs over, the one named last changes fastest.
Arguments:
- lower: bfloat16 [32, 3, 512, 2, 512], P('row', None, None, None, 'col'), as said below
- rhs: bfloat16 [32, 3, 512, 8192], P('row', None, None, 'col'), may hold values from -6 to 6
- tile_map: int32 [16], replicated, may hold values from 0 to 15, each once
Outputs:
- overwritten: bfloat16 [32, 3, 512, 8192], P('row', None, None, 'col')
Inputs may be any that keep to these rules, and one draw needn't show every extreme that they name: tile_map is a permutation of 0 to 15. lower[0, 0, :, 0, :] and lower[1, 0, :, 1, :] are lower triangular with diagonal entries between 2 and 3; lower[0, 0, :, 1, :] is zero.
All inputs are finite; a program needn't handle non-finite values.
Results may differ from a plain program's by a relative error of at most 0.0032.
Values may be sent and summed in bfloat16 or wider, within the bound.
A program may use at most 64 MiB of HBM per device.

v0:
```python
import jax
import jax.numpy as jnp
from jax import lax
from jax.sharding import Mesh
from jax.sharding import PartitionSpec as P

ROW = ("row_0", "row_1")


def spread(shard, axes, root):
    shard = jnp.where(lax.axis_index(axes) == root, shard, jnp.zeros_like(shard))
    for axis in axes:
        shard = lax.psum(shard, axis)
    return shard


def reorder(block, tile_map, tile):
    shape = block.shape
    tiles = block.reshape(shape[:-1] + (shape[-1] // tile, tile))
    return jnp.take(tiles, tile_map, axis=3).reshape(shape)


def body(lower, rhs, tile_map):
    tile = lower.shape[2]
    here = lax.axis_index(ROW)
    whole = lax.all_gather(lower, "col", axis=4, tiled=True)
    panels = whole[0]
    rows = panels.shape[0] * tile
    rhs = lax.all_to_all(
        reorder(
            lax.all_to_all(rhs, "col", split_axis=2, concat_axis=3, tiled=True), tile_map, tile
        ),
        "col",
        split_axis=3,
        concat_axis=2,
        tiled=True,
    )
    work = rhs[0].astype(jnp.float32)
    identity = jnp.eye(tile, dtype=jnp.float32)
    solved_rows = []
    for panel in range(2):
        mine = jnp.where(
            here == panel, jnp.tril(panels[0, :, panel, :].astype(jnp.float32)), identity
        )
        local = jax.scipy.linalg.solve_triangular(mine, work[0], lower=True).astype(jnp.bfloat16)
        solved = spread(local, ROW, panel)
        flat = panels[:, :, panel, :].reshape(rows, tile)
        work = work - jnp.dot(flat, solved, preferred_element_type=jnp.float32).reshape(work.shape)
        solved_rows.append(solved)
    first, second = (solved_rows[0], solved_rows[1])
    result = work.astype(jnp.bfloat16)
    leading = jnp.where(here == 0, first, jnp.where(here == 1, second, result[0]))
    result = result.at[0].set(leading)[None]
    return result


def solution(mesh):
    torus = Mesh(mesh.devices.reshape(8, 4, mesh.shape["col"]), ("row_0", "row_1", "col"))
    return jax.shard_map(
        body,
        mesh=torus,
        in_specs=(P(ROW, None, None, None, "col"), P(ROW, None, None, "col"), P()),
        out_specs=P(ROW, None, None, "col"),
        check_vma=False,
    )
```

profile of v0, /device:TPU:8, one launch (start us, length us, event | category | flops | bytes accessed | tf_op | source)
XLA Modules:
  0.0 522.2 jit_solution(17489380718761430764)
XLA Ops:
  6.5 4.1 copy.38
  10.6 9.4 %all-to-all-start = ((bf16[1,3,512,512]{3,1,0,2:T(4,128)(2,1)}), bf16[1,3,512,512]{3,1,0,2:T(4,128)(2,1)S(1)}, u32[]{:S(2)}, u32[]{:S(2)}) async-start(bf16[1,3,512,512]{3,1,0,2:T(4,128)(2,1)} %copy.38), calls=%async_computation | async-start | bytes 4194304 | tf_op jit(solution)/shard_map/all_to_all | solution.py:31
  21.2 56.9 %all-to-all-done = bf16[1,3,512,512]{3,1,0,2:T(4,128)(2,1)S(1)} async-done(((bf16[1,3,512,512]{3,1,0,2:T(4,128)(2,1)}), bf16[1,3,512,512]{3,1,0,2:T(4,128)(2,1)S(1)}, u32[]{:S(2)}, u32[]{:S(2)}) %all-to-all-start) | async-done | bytes 1572896 | tf_op jit(solution)/shard_map/all_to_all | solution.py:31
  83.5 8.3 %copy.41 = bf16[1,3,32,8192]{2,1,0,3:T(4,128)(2,1)} copy(bf16[1,3,32,8192]{3,2,1,0:T(8,128)(2,1)S(1)} %broadcast_select_fusion) | data formatting | bytes 3145728 | tf_op jit(solution)/shard_map/jit(_take)/select_n | solution.py:20
  91.8 13.2 %reshape.163 = bf16[16,2,24576]{2,1,0:T(2,128)(2,1)} reshape(bf16[8192,1,3,32]{3,2,1,0:T(4,128)(2,1)} %bitcast.122) | data formatting | bytes 3145728
  105.0 8.1 %all-to-all-start.1 = ((bf16[16,2,24576]{2,1,0:T(2,128)(2,1)}), bf16[16,2,24576]{2,1,0:T(2,128)(2,1)}, u32[]{:S(2)}, u32[]{:S(2)}) async-start(bf16[16,2,24576]{2,1,0:T(2,128)(2,1)} %reshape.163), calls=%async_computation.1 | async-start | bytes 3145728 | tf_op jit(solution)/shard_map/all_to_all | solution.py:29
  113.4 7.0 %copy.45 = bf16[1,3,512,2,512]{4,2,3,1,0:T(8,128)(2,1)S(1)} copy(bf16[1,3,512,2,512]{2,3,1,0,4:T(2,128)(2,1)} %all-gather.2.cloned.1.call-done) | data formatting | bytes 6291456 | tf_op jit(solution)/shard_map/all_gather | solution.py:26
  122.7 11.5 %while.5 = (s32[]{:T(128)}, f32[512,512]{1,0:T(8,128)}, s32[4,2]{0,1:T(2,128)S(1)}, f32[4,128,128]{2,1,0:T(8,128)S(1)}, s32[]{:T(128)}) while((s32[]{:T(128)}, f32[512,512]{1,0:T(8,128)}, s32[4,2]{0,1:T(2,128)S(1)}, f32[4,128,128]{2,1,0:T(8,128)S(1)}, s32[]{:T(128)}) %tuple.41), condition=%wide.while_cond.1, body=%wide.while_body.1.sunk | while | flops 2 | bytes 131189 | solution.py:45
  134.3 39.3 %custom-call.4 = f32[4,128,128]{1,2,0:T(8,128)S(1)} custom-call(f32[4,128,128]{2,1,0:T(8,128)S(1)} %get-tuple-element.32), custom_call_target="InvertDiagBlocksLowerTriangular" | custom-call | tf_op jit(solution)/shard_map/jit(_solve_triangular)/triangular_solve | solution.py:45
  173.6 12.6 %reshape.164 = bf16[8192,1,3,32]{3,2,1,0:T(4,128)(2,1)} reshape(bf16[16,2,24576]{2,1,0:T(2,128)(2,1)} %all-to-all-done.1) | data formatting | bytes 3145728
  186.2 9.7 %copy.42 = bf16[1,3,32,8192]{3,2,1,0:T(8,128)(2,1)S(1)} copy(bf16[1,3,32,8192]{2,1,0,3:T(4,128)(2,1)} %bitcast.123) | data formatting | bytes 3145728 | tf_op jit(solution)/shard_map/all_to_all | solution.py:29
  204.9 83.1 %all-reduce.5.cloned.1.call-done = bf16[512,512]{1,0:T(8,128)(2,1)} async-done(((bf16[512,512]{1,0:T(8,128)(2,1)}), bf16[512,512]{1,0:T(8,128)(2,1)}) %all-reduce.5.cloned.1.call-update) | async-done | bytes 524304 | tf_op jit(solution)/shard_map/psum | solution.py:13
  289.0 13.6 %while.6 = (s32[]{:T(128)}, f32[512,512]{1,0:T(8,128)}, s32[4,2]{0,1:T(2,128)S(1)}, f32[4,128,128]{2,1,0:T(8,128)}, s32[]{:T(128)}) while((s32[]{:T(128)}, f32[512,512]{1,0:T(8,128)}, s32[4,2]{0,1:T(2,128)S(1)}, f32[4,128,128]{2,1,0:T(8,128)}, s32[]{:T(128)}) %tuple.57), condition=%wide.while_cond.1.clone, body=%wide.while_body.1.clone.sunk | while | flops 2 | bytes 132205 | solution.py:45
  289.6 2.8 bitcast_dynamic-update-slice_fusion.5
  302.6 3.7 copy.43
  306.3 40.1 %custom-call.5 = f32[4,128,128]{1,2,0:T(8,128)S(1)} custom-call(f32[4,128,128]{2,1,0:T(8,128)} %get-tuple-element.33), custom_call_target="InvertDiagBlocksLowerTriangular" | custom-call | tf_op jit(solution)/shard_map/jit(_solve_triangular)/triangular_solve | solution.py:45
  346.4 4.0 fusion.50
  350.4 4.3 convolution_bitcast_fusion.1
  354.7 3.6 copy.47
  368.1 77.8 %all-reduce.9.cloned.1.call-done = bf16[512,512]{1,0:T(8,128)(2,1)} async-done(((bf16[512,512]{1,0:T(8,128)(2,1)}), bf16[512,512]{1,0:T(8,128)(2,1)}) %all-reduce.9.cloned.1.call-update) | async-done | bytes 524304 | tf_op jit(solution)/shard_map/psum | solution.py:13
  445.9 54.0 %all-reduce.11.cloned.1.call-done = bf16[512,512]{1,0:T(8,128)(2,1)} async-done(((bf16[512,512]{1,0:T(8,128)(2,1)}), bf16[512,512]{1,0:T(8,128)(2,1)}) %all-reduce.11.cloned.1.call-update) | async-done | bytes 524304 | tf_op jit(solution)/shard_map/psum | solution.py:13
  499.9 4.3 convolution_bitcast_fusion
  504.2 3.6 copy.50
  507.8 5.2 fusion.1
  (88 shorter events, 53.6 us)
Async XLA Ops:
  10.6 9.5 %copy-start.5 = (bf16[1,3,512,2,32]{2,4,3,1,0:T(8,128)(2,1)S(1)}, bf16[1,3,512,2,32]{2,4,3,1,0:T(8,128)(2,1)}, u32[]{:S(2)}) copy-start(bf16[1,3,512,2,32]{2,4,3,1,0:T(8,128)(2,1)} %param.7) | copy-start | bytes 589828
  10.6 10.4 %copy-start.6 = (s32[16]{0:T(128)S(1)}, s32[16]{0:T(128)}, u32[]{:S(2)}) copy-start(s32[16]{0:T(128)} %param.9) | copy-start | bytes 196
  10.6 67.4 %all-to-all-start = ((bf16[1,3,512,512]{3,1,0,2:T(4,128)(2,1)}), bf16[1,3,512,512]{3,1,0,2:T(4,128)(2,1)S(1)}, u32[]{:S(2)}, u32[]{:S(2)}) async-start(bf16[1,3,512,512]{3,1,0,2:T(4,128)(2,1)} %copy.38), calls=%async_computation | async-start | bytes 4194304 | tf_op jit(solution)/shard_map/all_to_all | solution.py:31
  20.1 93.4 %all-gather.2.cloned.1.call-start = ((), (), s32[]{:S(2)}) async-start(), calls=%async_computation.2 | async-start | bytes 3342336 | tf_op jit(solution)/shard_map/all_gather | solution.py:26
  105.0 68.5 %all-to-all-start.1 = ((bf16[16,2,24576]{2,1,0:T(2,128)(2,1)}), bf16[16,2,24576]{2,1,0:T(2,128)(2,1)}, u32[]{:S(2)}, u32[]{:S(2)}) async-start(bf16[16,2,24576]{2,1,0:T(2,128)(2,1)} %reshape.163), calls=%async_computation.1 | async-start | bytes 3145728 | tf_op jit(solution)/shard_map/all_to_all | solution.py:29
  113.2 174.8 %all-reduce.5.cloned.1.call-start = ((), (), s32[]{:S(2)}) async-start(), calls=%async_computation.3 | async-start | bytes 1048576 | tf_op jit(solution)/shard_map/psum | solution.py:13
  120.5 2.2 copy-start
  196.5 1.7 copy-start.1
  204.9 145.5 %all-reduce.7.cloned.1.call-start = ((), (), s32[]{:S(2)}) async-start(), calls=%async_computation.4 | async-start | bytes 1048576 | tf_op jit(solution)/shard_map/psum | solution.py:13
  288.0 157.9 %all-reduce.9.cloned.1.call-start = ((), (), s32[]{:S(2)}) async-start(), calls=%async_computation.5 | async-start | bytes 1048576 | tf_op jit(solution)/shard_map/psum | solution.py:13
  360.9 1.8 copy-start.2
  367.8 132.1 %all-reduce.11.cloned.1.call-start = ((), (), s32[]{:S(2)}) async-start(), calls=%async_computation.6 | async-start | bytes 1048576 | tf_op jit(solution)/shard_map/psum | solution.py:13
  507.8 5.2 copy-start.3
  507.8 5.2 copy-start.4
Sparse Core Ops, SparseCore 0:
  23.0 65.0 all-gather.1
  205.0 82.9 all-reduce.4
  290.4 51.8 all-reduce.6
  367.9 77.9 all-reduce.8
  448.1 51.7 all-reduce.10
where the time goes:
time: 524 us; the launch traced here: 522 us
  waiting for transfers between devices  272 us (52%)
  local copies, waits for them, and re-layouts  104 us (20%)
  other arithmetic  93.7 us (18%)
  matrix products  20.2 us (4%)
  starting transfers between devices  18.4 us (4%)
  between operations  13.5 us (3%)
    psum x4, waiting for transfers between devices, spread(): shard = lax.psum(shard, axis)  215 us
    another operation x4, other arithmetic, body(): jax.scipy.linalg.solve_triangular(mine, work[0], lower=True)  81.2 us
    all_to_all x1, waiting for transfers between devices, body(): lax.all_to_all(rhs, 'col', split_axis=2, concat_axis=3, tiled=True)  56.9 us
    unnamed x21, local copies, waits for them, and re-layouts  32.9 us
    another operation x27, local copies, waits for them, and re-layouts, body(): jax.scipy.linalg.solve_triangular(mine, work[0], lower=True)  25.7 us
    another operation x14, matrix products, body(): jax.scipy.linalg.solve_triangular(mine, work[0], lower=True)  11.6 us
  transfers between devices with their start and end apart: 7, of which 4 were waited for; matrix products, arithmetic and copies ran while one was open for 29% of the time, Pallas kernels for 0%

commit v1 on v0

--- a/solution.py
+++ b/solution.py
@@ -26,14 +26,24 @@
     whole = lax.all_gather(lower, "col", axis=4, tiled=True)
     panels = whole[0]
     rows = panels.shape[0] * tile
-    rhs = lax.all_to_all(
-        reorder(
-            lax.all_to_all(rhs, "col", split_axis=2, concat_axis=3, tiled=True), tile_map, tile
+    rhs = jnp.concatenate(
+        lax.all_to_all(
+            jnp.stack(
+                jnp.split(
+                    reorder(
+                        lax.all_to_all(rhs, "col", split_axis=2, concat_axis=3, tiled=True),
+                        tile_map,
+                        tile,
+                    ),
+                    lax.axis_size("col"),
+                    axis=3,
+                )
+            ),
+            "col",
+            0,
+            0,
         ),
-        "col",
-        split_axis=3,
-        concat_axis=2,
-        tiled=True,
+        axis=2,
     )
     work = rhs[0].astype(jnp.float32)
     identity = jnp.eye(tile, dtype=jnp.float32)

time: 524 us -> 531 us (1.013)
  waiting for transfers between devices: 272 us -> 307 us
  local copies, waits for them, and re-layouts: 104 us -> 75.6 us
    all_to_all x1, waiting for transfers between devices: 0.01 us -> 35.6 us  [body(): lax.all_to_all(jnp.stack(jnp.split(reorder(lax.all_to_all(rhs, 'col', spl...]
    unnamed x21 -> x37, local copies, waits for them, and re-layouts: 32.9 us -> 18.2 us
    all_to_all x2 -> x0, local copies, waits for them, and re-layouts: 11.2 us -> none  [the longest x1 9.68 us: body(): lax.all_to_all(reorder(lax.all_to_all(rhs, 'col', split_axis=2, concat_ax...]
    select_n x1 -> x0, local copies, waits for them, and re-layouts: 8.34 us -> none  [reorder(): return jnp.take(tiles, tile_map, axis=3).reshape(shape)]
  transfers between devices with their start and end apart: 7 -> 7, of which waited for: 4 -> 5; matrix products, arithmetic and copies ran while one was open for 29% -> 16% of each run, Pallas kernels for 0% -> 0%
where the time goes in v1:
time: 531 us; the launch traced here: 530 us
  waiting for transfers between devices  307 us (58%)
  other arithmetic  94.3 us (18%)
  local copies, waits for them, and re-layouts  75.6 us (14%)
  matrix products  21.3 us (4%)
  starting transfers between devices  18.1 us (3%)
  between operations  13.5 us (3%)
    psum x4, waiting for transfers between devices, spread(): shard = lax.psum(shard, axis)  215 us
    another operation x4, other arithmetic, body(): jax.scipy.linalg.solve_triangular(mine, work[0], lower=True)  81.4 us
    all_to_all x1, waiting for transfers between devices, body(): lax.all_to_all(rhs, 'col', split_axis=2, concat_axis=3, tiled=True)  56.9 us
    all_to_all x1, waiting for transfers between devices, body(): lax.all_to_all(jnp.stack(jnp.split(reorder(lax.all_to_all(rhs, 'col', spl...  35.6 us
    another operation x27, local copies, waits for them, and re-layouts, body(): jax.scipy.linalg.solve_triangular(mine, work[0], lower=True)  26.5 us
    unnamed x37, local copies, waits for them, and re-layouts  18.2 us
    another operation x14, matrix products, body(): jax.scipy.linalg.solve_triangular(mine, work[0], lower=True)  12.7 us
  transfers between devices with their start and end apart: 7, of which 5 were waited for; matrix products, arithmetic and copies ran while one was open for 16% of the time, Pallas kernels for 0%

profile of v1, /device:TPU:8, one launch (start us, length us, event | category | flops | bytes accessed | tf_op | source)
XLA Modules:
  0.0 530.1 jit_solution(9688891220978987260)
XLA Ops:
  6.5 4.1 copy.46
  10.6 9.4 %all-to-all-start = ((bf16[1,3,512,512]{3,1,0,2:T(4,128)(2,1)}), bf16[1,3,512,512]{3,1,0,2:T(4,128)(2,1)S(1)}, u32[]{:S(2)}, u32[]{:S(2)}) async-start(bf16[1,3,512,512]{3,1,0,2:T(4,128)(2,1)} %copy.46), calls=%async_computation | async-start | bytes 4194304 | tf_op jit(solution)/shard_map/all_to_all | solution.py:34
  21.2 56.9 %all-to-all-done = bf16[1,3,512,512]{3,1,0,2:T(4,128)(2,1)S(1)} async-done(((bf16[1,3,512,512]{3,1,0,2:T(4,128)(2,1)}), bf16[1,3,512,512]{3,1,0,2:T(4,128)(2,1)S(1)}, u32[]{:S(2)}, u32[]{:S(2)}) %all-to-all-start) | async-done | bytes 1572896 | tf_op jit(solution)/shard_map/all_to_all | solution.py:34
  79.4 4.0 gather_fusion
  98.8 8.1 %all-to-all-start.1 = ((bf16[16,1,3,32,512]{4,3,2,1,0:T(8,128)(2,1)}), bf16[16,1,3,32,512]{4,3,2,1,0:T(8,128)(2,1)S(1)}, u32[]{:S(2)}, u32[]{:S(2)}) async-start(bf16[16,1,3,32,512]{4,3,2,1,0:T(8,128)(2,1)} %fusion.36), calls=%async_computation.1 | async-start | bytes 3145728 | tf_op jit(solution)/shard_map/all_to_all | solution.py:30
  107.1 35.6 %all-to-all-done.1 = bf16[16,1,3,32,512]{4,3,2,1,0:T(8,128)(2,1)S(1)} async-done(((bf16[16,1,3,32,512]{4,3,2,1,0:T(8,128)(2,1)}), bf16[16,1,3,32,512]{4,3,2,1,0:T(8,128)(2,1)S(1)}, u32[]{:S(2)}, u32[]{:S(2)}) %all-to-all-start.1) | async-done | bytes 1572896 | tf_op jit(solution)/shard_map/all_to_all | solution.py:30
  145.9 7.0 %copy.50 = bf16[1,3,512,2,512]{4,2,3,1,0:T(8,128)(2,1)S(1)} copy(bf16[1,3,512,2,512]{2,3,1,0,4:T(2,128)(2,1)} %all-gather.2.cloned.1.call-done) | data formatting | bytes 6291456 | tf_op jit(solution)/shard_map/all_gather | solution.py:26
  155.3 11.5 %while.5 = (s32[]{:T(128)}, f32[512,512]{1,0:T(8,128)}, s32[4,2]{0,1:T(2,128)S(1)}, f32[4,128,128]{2,1,0:T(8,128)S(1)}, s32[]{:T(128)}) while((s32[]{:T(128)}, f32[512,512]{1,0:T(8,128)}, s32[4,2]{0,1:T(2,128)S(1)}, f32[4,128,128]{2,1,0:T(8,128)S(1)}, s32[]{:T(128)}) %tuple.41), condition=%wide.while_cond.1, body=%wide.while_body.1.sunk | while | flops 2 | bytes 131189 | solution.py:55
  166.8 39.3 %custom-call.4 = f32[4,128,128]{1,2,0:T(8,128)S(1)} custom-call(f32[4,128,128]{2,1,0:T(8,128)S(1)} %get-tuple-element.32), custom_call_target="InvertDiagBlocksLowerTriangular" | custom-call | tf_op jit(solution)/shard_map/jit(_solve_triangular)/triangular_solve | solution.py:55
  214.0 82.7 %all-reduce.5.cloned.1.call-done = bf16[512,512]{1,0:T(8,128)(2,1)} async-done(((bf16[512,512]{1,0:T(8,128)(2,1)}), bf16[512,512]{1,0:T(8,128)(2,1)}) %all-reduce.5.cloned.1.call-update) | async-done | bytes 524304 | tf_op jit(solution)/shard_map/psum | solution.py:13
  297.7 14.3 %while.6 = (s32[]{:T(128)}, f32[512,512]{1,0:T(8,128)}, s32[4,2]{0,1:T(2,128)S(1)}, f32[4,128,128]{2,1,0:T(8,128)}, s32[]{:T(128)}) while((s32[]{:T(128)}, f32[512,512]{1,0:T(8,128)}, s32[4,2]{0,1:T(2,128)S(1)}, f32[4,128,128]{2,1,0:T(8,128)}, s32[]{:T(128)}) %tuple.57), condition=%wide.while_cond.1.clone, body=%wide.while_body.1.clone.sunk | while | flops 2 | bytes 132205 | solution.py:55
  298.4 2.9 bitcast_dynamic-update-slice_fusion.5
  302.0 2.9 bitcast_dynamic-update-slice_fusion.5
  305.6 2.9 bitcast_dynamic-update-slice_fusion.5
  309.2 2.9 bitcast_dynamic-update-slice_fusion.5
  314.3 40.1 %custom-call.5 = f32[4,128,128]{1,2,0:T(8,128)S(1)} custom-call(f32[4,128,128]{2,1,0:T(8,128)} %get-tuple-element.33), custom_call_target="InvertDiagBlocksLowerTriangular" | custom-call | tf_op jit(solution)/shard_map/jit(_solve_triangular)/triangular_solve | solution.py:55
  354.4 4.0 fusion.66
  358.4 4.3 convolution_bitcast_fusion.1
  362.7 3.6 copy.51
  375.8 78.1 %all-reduce.9.cloned.1.call-done = bf16[512,512]{1,0:T(8,128)(2,1)} async-done(((bf16[512,512]{1,0:T(8,128)(2,1)}), bf16[512,512]{1,0:T(8,128)(2,1)}) %all-reduce.9.cloned.1.call-update) | async-done | bytes 524304 | tf_op jit(solution)/shard_map/psum | solution.py:13
  453.9 54.0 %all-reduce.11.cloned.1.call-done = bf16[512,512]{1,0:T(8,128)(2,1)} async-done(((bf16[512,512]{1,0:T(8,128)(2,1)}), bf16[512,512]{1,0:T(8,128)(2,1)}) %all-reduce.11.cloned.1.call-update) | async-done | bytes 524304 | tf_op jit(solution)/shard_map/psum | solution.py:13
  507.9 4.3 convolution_bitcast_fusion
  512.1 3.6 copy.54
  515.8 5.2 fusion.1
  (102 shorter events, 60.9 us)
Async XLA Ops:
  10.6 9.5 %copy-start.7 = (bf16[1,3,512,2,32]{2,4,3,1,0:T(8,128)(2,1)S(1)}, bf16[1,3,512,2,32]{2,4,3,1,0:T(8,128)(2,1)}, u32[]{:S(2)}) copy-start(bf16[1,3,512,2,32]{2,4,3,1,0:T(8,128)(2,1)} %param.7) | copy-start | bytes 589828
  10.6 10.4 %copy-start.8 = (s32[16]{0:T(128)S(1)}, s32[16]{0:T(128)}, u32[]{:S(2)}) copy-start(s32[16]{0:T(128)} %param.9) | copy-start | bytes 196
  10.6 67.4 %all-to-all-start = ((bf16[1,3,512,512]{3,1,0,2:T(4,128)(2,1)}), bf16[1,3,512,512]{3,1,0,2:T(4,128)(2,1)S(1)}, u32[]{:S(2)}, u32[]{:S(2)}) async-start(bf16[1,3,512,512]{3,1,0,2:T(4,128)(2,1)} %copy.46), calls=%async_computation | async-start | bytes 4194304 | tf_op jit(solution)/shard_map/all_to_all | solution.py:34
  20.1 125.8 %all-gather.2.cloned.1.call-start = ((), (), s32[]{:S(2)}) async-start(), calls=%async_computation.2 | async-start | bytes 3342336 | tf_op jit(solution)/shard_map/all_gather | solution.py:26
  78.1 1.3 copy-start.3
  98.8 44.0 %all-to-all-start.1 = ((bf16[16,1,3,32,512]{4,3,2,1,0:T(8,128)(2,1)}), bf16[16,1,3,32,512]{4,3,2,1,0:T(8,128)(2,1)S(1)}, u32[]{:S(2)}, u32[]{:S(2)}) async-start(bf16[16,1,3,32,512]{4,3,2,1,0:T(8,128)(2,1)} %fusion.36), calls=%async_computation.1 | async-start | bytes 3145728 | tf_op jit(solution)/shard_map/all_to_all | solution.py:30
  106.9 189.8 %all-reduce.5.cloned.1.call-start = ((), (), s32[]{:S(2)}) async-start(), calls=%async_computation.3 | async-start | bytes 1048576 | tf_op jit(solution)/shard_map/psum | solution.py:13
  143.2 1.7 copy-start
  152.9 2.4 copy-start.1
  155.3 54.0 %copy-start.4 = (f32[1,1,16,32,512]{4,3,1,0,2:T(8,128)S(1)}, f32[1,1,16,32,512]{4,3,1,0,2:T(8,128)}, u32[]{:S(2)}) copy-start(f32[1,1,16,32,512]{4,3,1,0,2:T(8,128)} %slice.87) | copy-start | bytes 3145732
  214.0 144.4 %all-reduce.7.cloned.1.call-start = ((), (), s32[]{:S(2)}) async-start(), calls=%async_computation.4 | async-start | bytes 1048576 | tf_op jit(solution)/shard_map/psum | solution.py:13
  296.7 157.2 %all-reduce.9.cloned.1.call-start = ((), (), s32[]{:S(2)}) async-start(), calls=%async_computation.5 | async-start | bytes 1048576 | tf_op jit(solution)/shard_map/psum | solution.py:13
  368.9 1.8 copy-start.2
  375.8 132.1 %all-reduce.11.cloned.1.call-start = ((), (), s32[]{:S(2)}) async-start(), calls=%async_computation.6 | async-start | bytes 1048576 | tf_op jit(solution)/shard_map/psum | solution.py:13
  515.7 5.2 copy-start.5
  515.7 5.2 copy-start.6
Sparse Core Ops, SparseCore 0:
  23.0 65.0 all-gather.1
  214.1 82.5 all-reduce.4
  299.1 52.2 all-reduce.6
  375.9 77.9 all-reduce.8
  456.1 51.7 all-reduce.10
